TPU v7x, 32 devices: a whole 2x2x4 slice. The times are simulated.
32 devices in a mesh: grp: 8 (over z, x), tp: 4 (over y, core).
Axes of the slice: x: 2, y: 2, z: 4, core: 2. Of those that a mesh axis runs over, the one named last changes fastest.
Arguments:
- prefix_keys: bfloat16 [16, 128, 1024], P(None, ('grp', 'tp')), may hold values from -4.5 to 4.5
- prefix_values: bfloat16 [16, 128, 1024], P(None, ('grp', 'tp')), may hold values from -24 to 24
- cand_queries: bfloat16 [8, 4, 256, 8192], P('grp', None, None, 'tp'), may hold values from -120 to 120
- cand_keys: bfloat16 [8, 4, 256, 1024], P('grp', None, None, 'tp'), may hold values from -4.2 to 4.2
- cand_values: bfloat16 [8, 4, 256, 1024], P('grp', None, None, 'tp'), may hold values from -24 to 24
- live_counts: int32 [8], replicated, may hold values from 1 to 4, as said below
- assignment: int32 [8], replicated, may hold values from 0 to 15
Outputs:
- attended: bfloat16 [8, 4, 256, 8192], P('grp', None, None, 'tp')
Inputs may be any that keep to these rules, and one draw needn't show every extreme that they name: The live passages of group g fill slots 0 to live_counts[g] - 1; some group has 4, and the group whose index differs from it in the lowest bit has 1.
All inputs are finite; a program needn't handle non-finite values.
Results may differ from a plain program's by a relative error of at most 0.0045.
Values may be sent and summed in bfloat16 or wider, within the bound.
No kernel may reach another device: no remote copies, remote signals or barrier semaphores. Data moves between devices by JAX's collectives and lax.ppermute only.
A program may use at most 64 MiB of HBM per device.

v0:
```python
import math

import jax
import jax.numpy as jnp
from jax import lax
from jax.sharding import PartitionSpec as P

HEAD_DIM = 128


masked_score = -1e30


def group_scores(query_block, key_block):
    scores = jnp.einsum(
        "pgrd,kgd->grpk", query_block, key_block, preferred_element_type=jnp.float32
    )
    return scores * (1.0 / math.sqrt(HEAD_DIM))


def mix_values(weights, value_block):
    return jnp.einsum(
        "grpk,kgd->pgrd",
        weights.astype(jnp.bfloat16),
        value_block,
        preferred_element_type=jnp.float32,
    )


def as_rows(stat):
    return jnp.moveaxis(stat, 2, 0)[..., None]


def run_span(slot_fn, starts, first, last):

    def advance(slot, buffers):
        results = slot_fn(slot)
        return tuple(
            (
                lax.dynamic_update_index_in_dim(buffer, result.astype(buffer.dtype), slot, 0)
                for buffer, result in zip(buffers, results)
            )
        )

    return lax.fori_loop(first, last, advance, starts)


def slot_blocks(data, slot, kv_local):
    queries, own_keys, own_values = data
    passage = queries.shape[1]
    query_block = lax.dynamic_index_in_dim(queries, slot, 0, keepdims=False).reshape(
        passage, kv_local, -1, HEAD_DIM
    )
    key_block = lax.dynamic_index_in_dim(own_keys, slot, 0, keepdims=False).reshape(
        passage, kv_local, HEAD_DIM
    )
    value_block = lax.dynamic_index_in_dim(own_values, slot, 0, keepdims=False).reshape(
        passage, kv_local, HEAD_DIM
    )
    return (query_block, key_block, value_block)


def per_device(
    prefix_keys, prefix_values, cand_queries, cand_keys, cand_values, live_counts, assignment
):
    slots = cand_queries.shape[1]
    passage = cand_queries.shape[2]
    q_width = cand_queries.shape[3]
    k_width = cand_keys.shape[3]
    kv_local = k_width // HEAD_DIM
    group = lax.axis_index("grp")
    count = live_counts[group]
    row_index = jnp.arange(passage, dtype=jnp.int32)
    causal = row_index[None, :] <= row_index[:, None]
    own_data = (cand_queries[0], cand_keys[0], cand_values[0])
    picked_keys = jnp.take(prefix_keys, assignment, axis=0)
    picked_values = jnp.take(prefix_values, assignment, axis=0)
    front_keys, front_values = (
        lax.all_to_all(
            lax.all_to_all(picked_keys, "grp", split_axis=0, concat_axis=1, tiled=True),
            "tp",
            split_axis=2,
            concat_axis=1,
            tiled=True,
        ),
        lax.all_to_all(
            lax.all_to_all(picked_values, "grp", split_axis=0, concat_axis=1, tiled=True),
            "tp",
            split_axis=2,
            concat_axis=1,
            tiled=True,
        ),
    )
    prefix_len = front_keys.shape[1]
    fronts = (
        front_keys[0].reshape(prefix_len, kv_local, HEAD_DIM),
        front_values[0].reshape(prefix_len, kv_local, HEAD_DIM),
    )

    def joint_slot(data, front_pair):

        def slot_fn(slot):
            query_block, key_block, value_block = slot_blocks(data, slot, kv_local)
            far_scores = group_scores(query_block, front_pair[0])
            near_scores = jnp.where(
                causal[None, None], group_scores(query_block, key_block), masked_score
            )
            peak = jnp.maximum(jnp.max(far_scores, axis=-1), jnp.max(near_scores, axis=-1))
            far_weights = jnp.exp(far_scores - peak[..., None])
            near_weights = jnp.exp(near_scores - peak[..., None])
            total = jnp.sum(far_weights, axis=-1) + jnp.sum(near_weights, axis=-1)
            mixed = mix_values(far_weights, front_pair[1]) + mix_values(near_weights, value_block)
            return ((mixed / as_rows(total)).reshape(passage, q_width),)

        return slot_fn

    own_fn = joint_slot(own_data, fronts)
    attended = run_span(own_fn, (jnp.zeros((slots, passage, q_width), jnp.bfloat16),), 0, slots)[0]
    alive = jnp.arange(slots, dtype=jnp.int32) < count
    attended = jnp.where(alive[:, None, None], attended, jnp.zeros_like(attended))
    return attended[None]


def solution(mesh):
    placed = (
        P(None, ("grp", "tp"), None),
        P(None, ("grp", "tp"), None),
        P("grp", None, None, "tp"),
        P("grp", None, None, "tp"),
        P("grp", None, None, "tp"),
        P(),
        P(),
    )
    return jax.shard_map(
        per_device,
        mesh=mesh,
        in_specs=placed,
        out_specs=P("grp", None, None, "tp"),
        check_vma=False,
    )
```

profile of v0, /device:TPU:0, one launch (start us, length us, event | category | flops | bytes accessed | tf_op | source)
XLA Modules:
  0.0 83.7 jit_solution(6182586386657871771)
XLA Ops:
  0.0 0.7 compare_select_fusion
  0.7 0.7 compare_and_fusion
  1.4 0.6 gather_fusion.1
  2.0 1.5 %gather_fusion = bf16[8,4,1024]{2,1,0:T(4,128)(2,1)S(1)} fusion(bf16[16,4,1024]{2,1,0:T(4,128)(2,1)} %param.11, s32[1024]{0:T(1024)S(1)} %pad_clamp_fusion), kind=kCustom, calls=%fused_computation.clone | custom fusion | bytes 131104 | tf_op jit(solution)/shard_map/jit(_take)/gather | solution.py:76
  3.5 0.8 broadcast_select_fusion
  4.3 14.0 %all_to_all.54 = bf16[8,4,1024]{2,1,0:T(4,128)(2,1)S(1)} all-to-all(bf16[8,4,1024]{2,1,0:T(4,128)(2,1)S(1)} %get-tuple-element.218), channel_id=1, replica_groups=mesh['grp'=8,'tp'=4] {'grp'}, dimensions={0} | all-to-all | bytes 131072 | tf_op jit(solution)/shard_map/all_to_all | solution.py:80
  18.2 3.4 %all-to-all-start.2 = ((bf16[8,4,1024]{2,1,0:T(4,128)(2,1)}), bf16[8,4,1024]{2,1,0:T(4,128)(2,1)S(1)}, u32[]{:S(2)}, u32[]{:S(2)}) async-start(bf16[8,4,1024]{2,1,0:T(4,128)(2,1)} %get-tuple-element.217), calls=%async_computation.2 | async-start | bytes 131072 | tf_op jit(solution)/shard_map/all_to_all | solution.py:87
  22.0 0.5 broadcast.78
  22.6 2.2 %reduce = bf16[1024,32]{1,0:T(8,128)(2,1)S(1)} reduce(bf16[1024,1,32]{2,1,0:T(2,128)(2,1)S(1)} %bitcast.140, bf16[]{:T(256)} %broadcast.78), dimensions={1}, to_apply=%bitcast.63.reduce_sub_computation | reduce | bytes 131074
  24.8 0.9 %reshape.97 = bf16[4,2,4096]{2,1,0:T(2,128)(2,1)} reshape(bf16[1024,32]{1,0:T(8,128)(2,1)S(1)} %reduce) | data formatting | bytes 131072
  25.7 2.7 %all-to-all-done.2 = bf16[8,4,1024]{2,1,0:T(4,128)(2,1)S(1)} async-done(((bf16[8,4,1024]{2,1,0:T(4,128)(2,1)}), bf16[8,4,1024]{2,1,0:T(4,128)(2,1)S(1)}, u32[]{:S(2)}, u32[]{:S(2)}) %all-to-all-start.2) | async-done | bytes 65568 | tf_op jit(solution)/shard_map/all_to_all | solution.py:87
  28.4 3.3 %all-to-all-start.1 = ((bf16[4,2,4096]{2,1,0:T(2,128)(2,1)}), bf16[4,2,4096]{2,1,0:T(2,128)(2,1)S(1)}, u32[]{:S(2)}, u32[]{:S(2)}) async-start(bf16[4,2,4096]{2,1,0:T(2,128)(2,1)} %reshape.97), calls=%async_computation.1 | async-start | bytes 131072 | tf_op jit(solution)/shard_map/all_to_all | solution.py:79
  31.7 1.2 %dynamic_slice.26 = s32[1]{0:T(128)} dynamic-slice(s32[8]{0:T(128)} %param.16, s32[]{:T(128)S(6)} %select_n.33), dynamic_slice_sizes={1} | dynamic-slice | bytes 12 | tf_op jit(solution)/shard_map/dynamic_slice | solution.py:72
  33.4 2.2 %reduce.1 = bf16[1024,32]{1,0:T(8,128)(2,1)S(1)} reduce(bf16[1024,1,32]{2,1,0:T(2,128)(2,1)S(1)} %bitcast.141, bf16[]{:T(256)} %broadcast.78), dimensions={1}, to_apply=%bitcast.65.reduce_sub_computation | reduce | bytes 131074
  35.6 0.9 %reshape.99 = bf16[4,2,4096]{2,1,0:T(2,128)(2,1)} reshape(bf16[1024,32]{1,0:T(8,128)(2,1)S(1)} %reduce.1) | data formatting | bytes 131072
  36.6 3.3 %all-to-all-start.3 = ((bf16[4,2,4096]{2,1,0:T(2,128)(2,1)}), bf16[4,2,4096]{2,1,0:T(2,128)(2,1)S(1)}, u32[]{:S(2)}, u32[]{:S(2)}) async-start(bf16[4,2,4096]{2,1,0:T(2,128)(2,1)} %reshape.99), calls=%async_computation.3 | async-start | bytes 131072 | tf_op jit(solution)/shard_map/all_to_all | solution.py:86
  39.8 0.7 iota_compare_fusion.1
  40.5 6.3 %copy.63 = bf16[1,4,256,2048]{2,3,1,0:T(8,128)(2,1)} copy(bf16[1,4,256,2048]{3,2,1,0:T(8,128)(2,1)} %param.13) | data formatting | bytes 8388608 | tf_op args[2]
  48.9 30.2 %while.15 = (s32[]{:T(128)}, bf16[4,256,2048]{2,1,0:T(8,128)(2,1)}, bf16[4,256,2048]{1,2,0:T(8,128)(2,1)}, bf16[128,2,128]{2,0,1:T(8,128)(2,1)S(1)}, bf16[4,256,...) while((s32[]{:T(128)}, bf16[4,256,2048]{2,1,0:T(8,128)(2,1)}, ...), condition=%wide.region_5.7_spmd.clone.clone, body=%wide.region_0.6_spmd.clone.sunk.clone | while | flops 822665216 | bytes 33931360 | solution.py:45
  49.0 1.3 %constant_dynamic-slice_fusion.8 = bf16[1,256,2048]{1,2,0:T(8,128)(2,1)S(1)} fusion(bf16[4,256,2048]{1,2,0:T(8,128)(2,1)} %get-tuple-element.312, s32[]{:T(128)S(6)} %copy.94), kind=kLoop, calls=%fused_computation.31.clone.1.clone | loop fusion | bytes 2097156 | tf_op jit(solution)/shard_map/while/body/eval_jaxpr/jit(dynamic_index_in_dim)/dynamic_slice | solution.py:51
  50.3 0.9 %fusion.60 = (f32[2,8,256]{2,1,0:T(8,128)S(1)}, f32[2,256,256,8]{2,1,3,0:T(8,128)S(1)}) fusion(pred[256,256]{0,1:T(8,128)(4,1)S(1)} %iota_compare_fusion.4, bf16[256,2,128,1]{0,2,3,1:T(8,128)(2,1)S(1)} %bitcast.135, bf16[256,2,8,128]{0,3,2,1:T(8,128)(2,1)S(1)} %bitcast.130), kind=kOutput, calls=%fused_computation.7.clone.1.clone | convolution fusion | flops 271577088 | bytes 5455872 | tf_op jit(solution)/shard_map/while/body/eval_jaxpr/pgrd,kgd->grpk/dot_general | solution.py:15
  51.6 1.2 %fusion.61 = f32[2,128,8,256]{3,1,2,0:T(8,128)S(1)} fusion(bf16[256,2,128,1]{0,2,3,1:T(8,128)(2,1)S(1)} %bitcast.134, f32[2,256,256,8]{2,1,3,0:T(8,128)S(1)} %get-tuple-element.284, f32[2,8,256]{2,1,0:T(8,128)S(1)} %max.14, pred[256,256]{0,1:T(8,128)(4,1)S(1)} %iota_compare_fusion.4), kind=kOutput, calls=%fused_computation.8.clone.1.clone | convolution fusion | flops 272629760 | bytes 6504448 | tf_op jit(solution)/shard_map/while/body/eval_jaxpr/grpk,kgd->pgrd/dot_general | solution.py:22
  53.2 0.9 %fusion.63 = f32[2,8,256]{2,1,0:T(8,128)S(1)} fusion(f32[2,256,256,8]{2,1,3,0:T(8,128)S(1)} %get-tuple-element.284, f32[2,8,256]{2,1,0:T(8,128)S(1)} %max.14, pred[256,256]{0,1:T(8,128)(4,1)S(1)} %iota_compare_fusion.4), kind=kLoop, calls=%fused_computation.5.clone.1.clone | loop fusion | flops 4190208 | bytes 4292608 | tf_op jit(solution)/shard_map/while/body/eval_jaxpr/reduce_sum | solution.py:111
  54.1 0.7 fusion.64
  54.8 0.6 copy.90
  55.4 1.0 %constant_dynamic-update-slice_fusion.3 = bf16[4,256,2048]{2,1,0:T(8,128)(2,1)} fusion(bf16[4,256,2048]{2,1,0:T(8,128)(2,1)} %get-tuple-element.304, bf16[1,256,2048]{2,1,0:T(8,128)(2,1)S(1)} %copy.90, s32[]{:T(128)S(6)} %copy.94), kind=kLoop, calls=%fused_computation.28.clone.1.clone | loop fusion | bytes 2097156 | tf_op jit(solution)/shard_map/while/body/eval_jaxpr/jit(dynamic_update_index_in_dim)/dynamic_update_slice | solution.py:40
  56.5 1.3 %constant_dynamic-slice_fusion.8 = bf16[1,256,2048]{1,2,0:T(8,128)(2,1)S(1)} fusion(bf16[4,256,2048]{1,2,0:T(8,128)(2,1)} %get-tuple-element.312, s32[]{:T(128)S(6)} %copy.94), kind=kLoop, calls=%fused_computation.31.clone.1.clone | loop fusion | bytes 2097156 | tf_op jit(solution)/shard_map/while/body/eval_jaxpr/jit(dynamic_index_in_dim)/dynamic_slice | solution.py:51
  57.8 0.9 %fusion.60 = (f32[2,8,256]{2,1,0:T(8,128)S(1)}, f32[2,256,256,8]{2,1,3,0:T(8,128)S(1)}) fusion(pred[256,256]{0,1:T(8,128)(4,1)S(1)} %iota_compare_fusion.4, bf16[256,2,128,1]{0,2,3,1:T(8,128)(2,1)S(1)} %bitcast.135, bf16[256,2,8,128]{0,3,2,1:T(8,128)(2,1)S(1)} %bitcast.130), kind=kOutput, calls=%fused_computation.7.clone.1.clone | convolution fusion | flops 271577088 | bytes 5455872 | tf_op jit(solution)/shard_map/while/body/eval_jaxpr/pgrd,kgd->grpk/dot_general | solution.py:15
  59.1 1.2 %fusion.61 = f32[2,128,8,256]{3,1,2,0:T(8,128)S(1)} fusion(bf16[256,2,128,1]{0,2,3,1:T(8,128)(2,1)S(1)} %bitcast.134, f32[2,256,256,8]{2,1,3,0:T(8,128)S(1)} %get-tuple-element.284, f32[2,8,256]{2,1,0:T(8,128)S(1)} %max.14, pred[256,256]{0,1:T(8,128)(4,1)S(1)} %iota_compare_fusion.4), kind=kOutput, calls=%fused_computation.8.clone.1.clone | convolution fusion | flops 272629760 | bytes 6504448 | tf_op jit(solution)/shard_map/while/body/eval_jaxpr/grpk,kgd->pgrd/dot_general | solution.py:22
  60.7 0.9 %fusion.63 = f32[2,8,256]{2,1,0:T(8,128)S(1)} fusion(f32[2,256,256,8]{2,1,3,0:T(8,128)S(1)} %get-tuple-element.284, f32[2,8,256]{2,1,0:T(8,128)S(1)} %max.14, pred[256,256]{0,1:T(8,128)(4,1)S(1)} %iota_compare_fusion.4), kind=kLoop, calls=%fused_computation.5.clone.1.clone | loop fusion | flops 4190208 | bytes 4292608 | tf_op jit(solution)/shard_map/while/body/eval_jaxpr/reduce_sum | solution.py:111
  61.6 0.7 fusion.64
  62.3 0.6 copy.90
  63.0 1.0 %constant_dynamic-update-slice_fusion.3 = bf16[4,256,2048]{2,1,0:T(8,128)(2,1)} fusion(bf16[4,256,2048]{2,1,0:T(8,128)(2,1)} %get-tuple-element.304, bf16[1,256,2048]{2,1,0:T(8,128)(2,1)S(1)} %copy.90, s32[]{:T(128)S(6)} %copy.94), kind=kLoop, calls=%fused_computation.28.clone.1.clone | loop fusion | bytes 2097156 | tf_op jit(solution)/shard_map/while/body/eval_jaxpr/jit(dynamic_update_index_in_dim)/dynamic_update_slice | solution.py:40
  64.1 1.3 %constant_dynamic-slice_fusion.8 = bf16[1,256,2048]{1,2,0:T(8,128)(2,1)S(1)} fusion(bf16[4,256,2048]{1,2,0:T(8,128)(2,1)} %get-tuple-element.312, s32[]{:T(128)S(6)} %copy.94), kind=kLoop, calls=%fused_computation.31.clone.1.clone | loop fusion | bytes 2097156 | tf_op jit(solution)/shard_map/while/body/eval_jaxpr/jit(dynamic_index_in_dim)/dynamic_slice | solution.py:51
  65.4 0.9 %fusion.60 = (f32[2,8,256]{2,1,0:T(8,128)S(1)}, f32[2,256,256,8]{2,1,3,0:T(8,128)S(1)}) fusion(pred[256,256]{0,1:T(8,128)(4,1)S(1)} %iota_compare_fusion.4, bf16[256,2,128,1]{0,2,3,1:T(8,128)(2,1)S(1)} %bitcast.135, bf16[256,2,8,128]{0,3,2,1:T(8,128)(2,1)S(1)} %bitcast.130), kind=kOutput, calls=%fused_computation.7.clone.1.clone | convolution fusion | flops 271577088 | bytes 5455872 | tf_op jit(solution)/shard_map/while/body/eval_jaxpr/pgrd,kgd->grpk/dot_general | solution.py:15
  66.7 1.2 %fusion.61 = f32[2,128,8,256]{3,1,2,0:T(8,128)S(1)} fusion(bf16[256,2,128,1]{0,2,3,1:T(8,128)(2,1)S(1)} %bitcast.134, f32[2,256,256,8]{2,1,3,0:T(8,128)S(1)} %get-tuple-element.284, f32[2,8,256]{2,1,0:T(8,128)S(1)} %max.14, pred[256,256]{0,1:T(8,128)(4,1)S(1)} %iota_compare_fusion.4), kind=kOutput, calls=%fused_computation.8.clone.1.clone | convolution fusion | flops 272629760 | bytes 6504448 | tf_op jit(solution)/shard_map/while/body/eval_jaxpr/grpk,kgd->pgrd/dot_general | solution.py:22
  68.3 0.9 %fusion.63 = f32[2,8,256]{2,1,0:T(8,128)S(1)} fusion(f32[2,256,256,8]{2,1,3,0:T(8,128)S(1)} %get-tuple-element.284, f32[2,8,256]{2,1,0:T(8,128)S(1)} %max.14, pred[256,256]{0,1:T(8,128)(4,1)S(1)} %iota_compare_fusion.4), kind=kLoop, calls=%fused_computation.5.clone.1.clone | loop fusion | flops 4190208 | bytes 4292608 | tf_op jit(solution)/shard_map/while/body/eval_jaxpr/reduce_sum | solution.py:111
  69.2 0.7 fusion.64
  69.9 0.6 copy.90
  70.5 1.0 %constant_dynamic-update-slice_fusion.3 = bf16[4,256,2048]{2,1,0:T(8,128)(2,1)} fusion(bf16[4,256,2048]{2,1,0:T(8,128)(2,1)} %get-tuple-element.304, bf16[1,256,2048]{2,1,0:T(8,128)(2,1)S(1)} %copy.90, s32[]{:T(128)S(6)} %copy.94), kind=kLoop, calls=%fused_computation.28.clone.1.clone | loop fusion | bytes 2097156 | tf_op jit(solution)/shard_map/while/body/eval_jaxpr/jit(dynamic_update_index_in_dim)/dynamic_update_slice | solution.py:40
  71.6 1.3 %constant_dynamic-slice_fusion.8 = bf16[1,256,2048]{1,2,0:T(8,128)(2,1)S(1)} fusion(bf16[4,256,2048]{1,2,0:T(8,128)(2,1)} %get-tuple-element.312, s32[]{:T(128)S(6)} %copy.94), kind=kLoop, calls=%fused_computation.31.clone.1.clone | loop fusion | bytes 2097156 | tf_op jit(solution)/shard_map/while/body/eval_jaxpr/jit(dynamic_index_in_dim)/dynamic_slice | solution.py:51
  72.9 0.9 %fusion.60 = (f32[2,8,256]{2,1,0:T(8,128)S(1)}, f32[2,256,256,8]{2,1,3,0:T(8,128)S(1)}) fusion(pred[256,256]{0,1:T(8,128)(4,1)S(1)} %iota_compare_fusion.4, bf16[256,2,128,1]{0,2,3,1:T(8,128)(2,1)S(1)} %bitcast.135, bf16[256,2,8,128]{0,3,2,1:T(8,128)(2,1)S(1)} %bitcast.130), kind=kOutput, calls=%fused_computation.7.clone.1.clone | convolution fusion | flops 271577088 | bytes 5455872 | tf_op jit(solution)/shard_map/while/body/eval_jaxpr/pgrd,kgd->grpk/dot_general | solution.py:15
  74.3 1.2 %fusion.61 = f32[2,128,8,256]{3,1,2,0:T(8,128)S(1)} fusion(bf16[256,2,128,1]{0,2,3,1:T(8,128)(2,1)S(1)} %bitcast.134, f32[2,256,256,8]{2,1,3,0:T(8,128)S(1)} %get-tuple-element.284, f32[2,8,256]{2,1,0:T(8,128)S(1)} %max.14, pred[256,256]{0,1:T(8,128)(4,1)S(1)} %iota_compare_fusion.4), kind=kOutput, calls=%fused_computation.8.clone.1.clone | convolution fusion | flops 272629760 | bytes 6504448 | tf_op jit(solution)/shard_map/while/body/eval_jaxpr/grpk,kgd->pgrd/dot_general | solution.py:22
  75.8 0.9 %fusion.63 = f32[2,8,256]{2,1,0:T(8,128)S(1)} fusion(f32[2,256,256,8]{2,1,3,0:T(8,128)S(1)} %get-tuple-element.284, f32[2,8,256]{2,1,0:T(8,128)S(1)} %max.14, pred[256,256]{0,1:T(8,128)(4,1)S(1)} %iota_compare_fusion.4), kind=kLoop, calls=%fused_computation.5.clone.1.clone | loop fusion | flops 4190208 | bytes 4292608 | tf_op jit(solution)/shard_map/while/body/eval_jaxpr/reduce_sum | solution.py:111
  76.7 0.7 fusion.64
  77.4 0.6 copy.90
  78.1 1.0 %constant_dynamic-update-slice_fusion.3 = bf16[4,256,2048]{2,1,0:T(8,128)(2,1)} fusion(bf16[4,256,2048]{2,1,0:T(8,128)(2,1)} %get-tuple-element.304, bf16[1,256,2048]{2,1,0:T(8,128)(2,1)S(1)} %copy.90, s32[]{:T(128)S(6)} %copy.94), kind=kLoop, calls=%fused_computation.28.clone.1.clone | loop fusion | bytes 2097156 | tf_op jit(solution)/shard_map/while/body/eval_jaxpr/jit(dynamic_update_index_in_dim)/dynamic_update_slice | solution.py:40
  79.1 4.5 %select_bitcast_fusion = bf16[1,4,256,2048]{3,2,1,0:T(8,128)(2,1)} fusion(bf16[4,256,2048]{2,1,0:T(8,128)(2,1)} %get-tuple-element.145, pred[4]{0:T(512)(128)(4,1)S(1)} %iota_compare_fusion.1), kind=kLoop, calls=%fused_computation.35 | loop fusion | flops 2097152 | bytes 8388612 | tf_op jit(solution)/shard_map/broadcast_in_dim | solution.py:121
  (52 shorter events, 6.3 us)
Async XLA Ops:
  0.0 1.4 %copy-start = (bf16[16,4,1024]{2,1,0:T(4,128)(2,1)S(1)}, bf16[16,4,1024]{2,1,0:T(4,128)(2,1)}, u32[]{:S(2)}) copy-start(bf16[16,4,1024]{2,1,0:T(4,128)(2,1)} %param.12) | copy-start | bytes 393220
  18.2 10.2 %all-to-all-start.2 = ((bf16[8,4,1024]{2,1,0:T(4,128)(2,1)}), bf16[8,4,1024]{2,1,0:T(4,128)(2,1)S(1)}, u32[]{:S(2)}, u32[]{:S(2)}) async-start(bf16[8,4,1024]{2,1,0:T(4,128)(2,1)} %get-tuple-element.217), calls=%async_computation.2 | async-start | bytes 131072 | tf_op jit(solution)/shard_map/all_to_all | solution.py:87
  28.4 8.1 %all-to-all-start.1 = ((bf16[4,2,4096]{2,1,0:T(2,128)(2,1)}), bf16[4,2,4096]{2,1,0:T(2,128)(2,1)S(1)}, u32[]{:S(2)}, u32[]{:S(2)}) async-start(bf16[4,2,4096]{2,1,0:T(2,128)(2,1)} %reshape.97), calls=%async_computation.1 | async-start | bytes 131072 | tf_op jit(solution)/shard_map/all_to_all | solution.py:79
  36.6 11.5 %all-to-all-start.3 = ((bf16[4,2,4096]{2,1,0:T(2,128)(2,1)}), bf16[4,2,4096]{2,1,0:T(2,128)(2,1)S(1)}, u32[]{:S(2)}, u32[]{:S(2)}) async-start(bf16[4,2,4096]{2,1,0:T(2,128)(2,1)} %reshape.99), calls=%async_computation.3 | async-start | bytes 131072 | tf_op jit(solution)/shard_map/all_to_all | solution.py:86
  40.5 6.3 %copy-start.1 = (bf16[1,4,256,256]{3,2,1,0:T(8,128)(2,1)S(1)}, bf16[1,4,256,256]{3,2,1,0:T(8,128)(2,1)}, u32[]{:S(2)}) copy-start(bf16[1,4,256,256]{3,2,1,0:T(8,128)(2,1)} %param.14) | copy-start | bytes 1572868
  40.5 6.5 %copy-start.2 = (bf16[1,4,256,256]{3,2,1,0:T(8,128)(2,1)S(1)}, bf16[1,4,256,256]{3,2,1,0:T(8,128)(2,1)}, u32[]{:S(2)}) copy-start(bf16[1,4,256,256]{3,2,1,0:T(8,128)(2,1)} %param.15) | copy-start | bytes 1572868
where the time goes:
time: 84.5 us; the launch traced here: 83.7 us
  local copies, waits for them, and re-layouts  26.8 us (32%)
  other arithmetic  17 us (20%)
  blocking collectives  14 us (17%)
  matrix products  12.7 us (15%)
  starting transfers between devices  9.92 us (12%)
  waiting for transfers between devices  2.73 us (3%)
    all_to_all x1, blocking collectives, per_device(): lax.all_to_all(picked_keys, 'grp', split_axis=0, concat_axis=1, tiled=True)  14 us
    unnamed x16, local copies, waits for them, and re-layouts  9.94 us
    dot_general x8, matrix products, mix_values(): jnp.einsum('grpk,kgd->pgrd', weights.astype(jnp.bfloat16), value_block, p...  7.53 us
    dynamic_update_slice x8, local copies, waits for them, and re-layouts, advance(): lax.dynamic_update_index_in_dim(buffer, result.astype(buffer.dtype), slot...  6.75 us
    dynamic_slice x4, local copies, waits for them, and re-layouts, slot_blocks(): lax.dynamic_index_in_dim(queries, slot, 0, keepdims=False)  5.2 us
    dot_general x8, matrix products, group_scores(): jnp.einsum('pgrd,kgd->grpk', query_block, key_block, preferred_element_ty...  5.18 us
    reduce_sum x8, other arithmetic, slot_fn(): total = jnp.sum(far_weights, axis=-1) + jnp.sum(near_weights, axis=-1)  5.03 us
    broadcast_in_dim x1, other arithmetic, per_device(): return attended[None]  4.54 us
  transfers between devices with their start and end apart: 3, of which 1 were waited for; matrix products, arithmetic and copies ran while one was open for 20% of the time, Pallas kernels for 0%

commit v1 on v0

v1 whole, which is shorter than its diff:
```python
import math

import jax
import jax.numpy as jnp
from jax import lax
from jax.experimental import pallas as pl
from jax.experimental.pallas import tpu as pltpu
from jax.sharding import PartitionSpec as P

HEAD_DIM = 128
MASKED = -1e30
SCALE = math.log2(math.e) / math.sqrt(HEAD_DIM)
VMEM_LIMIT = 60 * 1024 * 1024
BF16 = jnp.bfloat16
F32 = jnp.float32
NEAR = jnp.float32


def dot_nt(a, b):
    return lax.dot_general(a, b, (((1,), (1,)), ((), ())), preferred_element_type=F32)


def dot_nn(a, b):
    return lax.dot_general(a, b, (((1,), (0,)), ((), ())), preferred_element_type=F32)


def pick_kernel(assign, keys, values, out, sem):
    tp = out.shape[0] // assign.shape[0]
    width = out.shape[3]

    def group(g, carry):
        row = assign[g]
        for t in range(tp):
            for i, src in enumerate((keys, values)):
                pltpu.make_async_copy(
                    src.at[row, :, pl.ds(t * width, width)], out.at[g * tp + t, i], sem
                ).start()
        return carry

    lax.fori_loop(0, assign.shape[0], group, 0)
    pltpu.make_async_copy(out, out, sem).wait()


def query_tile(q, i, pairs):
    d = HEAD_DIM
    return jnp.concatenate(
        [
            jnp.concatenate(
                [q[0, 0, :, p * d : (p + 1) * d], q[0, 0, :, (pairs + p) * d : (pairs + p + 1) * d]],
                axis=1,
            )
            for p in (2 * i, 2 * i + 1)
        ],
        axis=0,
    )


def near_kernel(counts, q, k, v, o, stat, kbd, vtd):
    count = counts[lax.axis_index("grp")]
    s, t = pl.program_id(0), pl.program_id(1)
    half = q.shape[2]
    pairs = q.shape[3] // (2 * HEAD_DIM)
    d = HEAD_DIM

    @pl.when((s == 0) & (t == 0))
    def _():
        kbd[...] = jnp.zeros_like(kbd)
        vtd[...] = jnp.zeros_like(vtd)

    @pl.when((s < count) & (t == 0))
    def _():
        vt = v[0, 0].T
        for b in range(2):
            rows = slice(b * half, (b + 1) * half)
            for h in range(2):
                at = slice((2 * b + h) * half, (2 * b + h + 1) * half)
                cols = slice(h * d, (h + 1) * d)
                kbd[at, cols] = k[0, 0, rows, cols]
                vtd[cols, at] = vt[cols, rows]

    def attend(blocks):
        row = lax.broadcasted_iota(jnp.int32, (half, 2 * half), 0)
        col = lax.broadcasted_iota(jnp.int32, (half, 2 * half), 1)
        seen = row <= jnp.where(col < half, col, col - half)
        keys = kbd[: blocks * 2 * half]
        mixers = vtd[:, : blocks * 2 * half]
        for i in range(pairs // 2):
            scores = dot_nt(keys, query_tile(q, i, pairs))
            weights = [None] * (2 * blocks)
            for h in range(2):
                parts = []
                for b in range(blocks):
                    x = scores[(2 * b + h) * half : (2 * b + h + 1) * half]
                    parts.append(jnp.where(seen, x, MASKED) if b == blocks - 1 else x)
                top = jnp.max(parts[0], axis=0, keepdims=True)
                for x in parts[1:]:
                    top = jnp.maximum(top, jnp.max(x, axis=0, keepdims=True))
                total = None
                for b, x in enumerate(parts):
                    e = jnp.exp2((x - top) * SCALE)
                    part = jnp.sum(e, axis=0, keepdims=True)
                    total = part if total is None else total + part
                    weights[2 * b + h] = e.astype(BF16)
                stat[0, 0, i, h : h + 1, :] = top
                stat[0, 0, i, 2 + h : 3 + h, :] = total
            o[0, 0, i] = dot_nn(mixers, jnp.concatenate(weights, axis=0)).astype(o.dtype)

    @pl.when((s < count) & (t == 0))
    def _():
        attend(1)

    @pl.when((s < count) & (t == 1))
    def _():
        attend(2)


def far_kernel(counts, front, q, o, stat, out, rows, kfd, vfd):
    count = counts[lax.axis_index("grp")]
    s, t = pl.program_id(0), pl.program_id(1)
    half = q.shape[2]
    pairs = q.shape[3] // (2 * HEAD_DIM)
    d = HEAD_DIM
    devices, _, local, _ = front.shape
    prefix = devices * local

    @pl.when((s == 0) & (t == 0))
    def _():
        kfd[...] = jnp.zeros_like(kfd)
        vfd[...] = jnp.zeros_like(vfd)
        for i in range(2):
            for n in range(devices):
                rows[i, n * local : (n + 1) * local, :] = front[n, i].astype(F32)
        for h in range(2):
            cols = slice(h * d, (h + 1) * d)
            at = slice(h * prefix, (h + 1) * prefix)
            kfd[at, cols] = rows[0, :, cols].astype(BF16)
            vfd[cols, at] = rows[1, :, cols].T.astype(BF16)

    @pl.when(s >= count)
    def _():
        out[...] = jnp.zeros_like(out)

    @pl.when(s < count)
    def _():
        for i in range(pairs // 2):
            scores = dot_nt(kfd[...], query_tile(q, i, pairs))
            weights, fades, invs = [], [], []
            for h in range(2):
                x = scores[h * prefix : (h + 1) * prefix]
                m = stat[0, 0, i, h : h + 1, :]
                l = stat[0, 0, i, 2 + h : 3 + h, :]
                top = jnp.maximum(m, jnp.max(x, axis=0, keepdims=True))
                e = jnp.exp2((x - top) * SCALE)
                fade = jnp.exp2((m - top) * SCALE)
                total = l * fade + jnp.sum(e, axis=0, keepdims=True)
                weights.append(e.astype(BF16))
                fades.append(fade)
                invs.append(1.0 / total)
            mixed = dot_nn(vfd[...], jnp.concatenate(weights, axis=0))
            for h in range(2):
                r = slice(h * d, (h + 1) * d)
                y = (mixed[r] + o[0, 0, i, r, :].astype(F32) * fades[h]) * invs[h]
                y = y.astype(BF16).T
                for n in range(2):
                    c = (h * pairs + 2 * i + n) * d
                    out[0, 0, :, c : c + d] = y[n * half : (n + 1) * half]


def per_device(
    prefix_keys, prefix_values, cand_queries, cand_keys, cand_values, live_counts, assignment
):
    _, slots, passage, q_width = cand_queries.shape
    k_width = cand_keys.shape[3]
    local = prefix_keys.shape[1]
    devices = lax.axis_size("grp") * lax.axis_size("tp")
    prefix = devices * local
    pairs = q_width // (2 * HEAD_DIM)
    assert k_width == 2 * HEAD_DIM
    any_space = pl.BlockSpec(memory_space=pl.ANY)
    vmem = pl.BlockSpec(memory_space=pltpu.VMEM)
    smem = pl.BlockSpec(memory_space=pltpu.SMEM)
    picked = pl.pallas_call(
        pick_kernel,
        out_shape=jax.ShapeDtypeStruct((devices, 2, local, k_width), BF16),
        in_specs=[smem, any_space, any_space],
        out_specs=any_space,
        scratch_shapes=[pltpu.SemaphoreType.DMA],
        compiler_params=pltpu.CompilerParams(vmem_limit_bytes=1024 * 1024),
        name="pick",
    )(assignment, prefix_keys, prefix_values)
    front = lax.all_to_all(picked, ("grp", "tp"), split_axis=0, concat_axis=0, tiled=True)

    half = passage // 2
    flops = 4 * slots * passage * q_width * passage
    tile = lambda s, t: (0, s, t, 0)
    whole = lambda s, t: (0, s, 0, 0)
    q_spec = pl.BlockSpec((1, 1, half, q_width), tile)
    kv_spec = pl.BlockSpec((1, 1, passage, k_width), whole)
    o_spec = pl.BlockSpec((1, 1, pairs // 2, k_width, 2 * half), lambda s, t: (s, t, 0, 0, 0))
    stat_spec = pl.BlockSpec((1, 1, pairs // 2, 8, 2 * half), lambda s, t: (s, t, 0, 0, 0))
    o, stat = pl.pallas_call(
        near_kernel,
        out_shape=(
            jax.ShapeDtypeStruct((slots, 2, pairs // 2, k_width, 2 * half), NEAR),
            jax.ShapeDtypeStruct((slots, 2, pairs // 2, 8, 2 * half), F32),
        ),
        grid=(slots, 2),
        in_specs=[smem, q_spec, kv_spec, kv_spec],
        out_specs=(o_spec, stat_spec),
        scratch_shapes=[
            pltpu.VMEM((2 * passage, k_width), BF16),
            pltpu.VMEM((k_width, 2 * passage), BF16),
        ],
        compiler_params=pltpu.CompilerParams(vmem_limit_bytes=VMEM_LIMIT),
        cost_estimate=pl.CostEstimate(flops=flops, transcendentals=0, bytes_accessed=0),
        name="near",
    )(live_counts, cand_queries, cand_keys, cand_values)

    return pl.pallas_call(
        far_kernel,
        out_shape=jax.ShapeDtypeStruct(cand_queries.shape, BF16),
        grid=(slots, 2),
        in_specs=[smem, vmem, q_spec, o_spec, stat_spec],
        out_specs=q_spec,
        scratch_shapes=[
            pltpu.VMEM((2, prefix, k_width), F32),
            pltpu.VMEM((2 * prefix, k_width), BF16),
            pltpu.VMEM((k_width, 2 * prefix), BF16),
        ],
        compiler_params=pltpu.CompilerParams(vmem_limit_bytes=VMEM_LIMIT),
        name="far",
    )(live_counts, front, cand_queries, o, stat)


def solution(mesh):
    placed = (
        P(None, ("grp", "tp"), None),
        P(None, ("grp", "tp"), None),
        P("grp", None, None, "tp"),
        P("grp", None, None, "tp"),
        P("grp", None, None, "tp"),
        P(),
        P(),
    )
    return jax.shard_map(
        per_device,
        mesh=mesh,
        in_specs=placed,
        out_specs=P("grp", None, None, "tp"),
        check_vma=False,
    )
```

time: 84.5 us -> 37.3 us (0.44)
  the two profiles are of different devices: /device:TPU:0 before, /device:TPU:19 now
where the time goes in v1:
time: 37.3 us; the launch traced here: 36.7 us
  Pallas kernels  27.4 us (73%)
  starting transfers between devices  6.2 us (17%)
  local copies, waits for them, and re-layouts  3.1 us (8%)
    pallas_call x1, Pallas kernels, per_device(): pl.pallas_call(near_kernel, out_shape=(jax.ShapeDtypeStruct((slots, 2, pa...  13.4 us
    pallas_call x1, Pallas kernels, per_device(): pl.pallas_call(far_kernel, out_shape=jax.ShapeDtypeStruct(cand_queries.sh...  12.7 us
    all_to_all x1, starting transfers between devices, per_device(): lax.all_to_all(picked, ('grp', 'tp'), split_axis=0, concat_axis=0, tiled=...  6.2 us
    unnamed x8, local copies, waits for them, and re-layouts  3.1 us
    pallas_call x1, Pallas kernels, per_device(): pl.pallas_call(pick_kernel, out_shape=jax.ShapeDtypeStruct((devices, 2, l...  1.36 us
  transfers between devices with their start and end apart: 1, of which 0 were waited for; matrix products, arithmetic and copies ran while one was open for 0% of the time, Pallas kernels for 36%

profile of v1, /device:TPU:19, one launch (start us, length us, event | category | flops | bytes accessed | tf_op | source)
XLA Modules:
  0.0 36.7 jit_solution(5198132960392884267)
XLA Ops:
  0.0 0.0 copy-start
  0.0 0.9 %copy-done = bf16[16,4,1024]{2,1,0:T(4,128)(2,1)S(1)} copy-done((bf16[16,4,1024]{2,1,0:T(4,128)(2,1)S(1)}, bf16[16,4,1024]{2,1,0:T(4,128)(2,1)}, u32[]{:S(2)}) %copy-start) | copy-done | bytes 131096
  0.9 0.0 copy-start.1
  0.9 0.9 %copy-done.1 = bf16[16,4,1024]{2,1,0:T(4,128)(2,1)S(1)} copy-done((bf16[16,4,1024]{2,1,0:T(4,128)(2,1)S(1)}, bf16[16,4,1024]{2,1,0:T(4,128)(2,1)}, u32[]{:S(2)}) %copy-start.1) | copy-done | bytes 131096
  1.8 0.0 copy-start.2
  1.8 0.7 %copy-done.2 = s32[8]{0:T(128)S(1)} copy-done((s32[8]{0:T(128)S(1)}, s32[8]{0:T(128)}, u32[]{:S(2)}) %copy-start.2) | copy-done | bytes 56
  2.5 1.4 %pick.1 = bf16[32,2,4,256]{3,2,1,0:T(4,128)(2,1)} custom-call(s32[8]{0:T(128)S(1)} %copy-done.2, bf16[16,4,1024]{2,1,0:T(4,128)(2,1)S(1)} %copy-done, bf16[16,4,1024]{2,1,0:T(4,128)(2,1)S(1)} %copy-done.1), custom_call_target="tpu_custom_call" | custom-call | tf_op jit(solution)/shard_map/pick/pallas_call | solution.py:182
  3.8 6.2 %all-to-all-start = ((bf16[32,2,4,256]{3,2,1,0:T(4,128)(2,1)}), bf16[32,2,4,256]{3,2,1,0:T(4,128)(2,1)S(1)}, u32[]{:S(2)}, u32[]{:S(2)}) async-start(bf16[32,2,4,256]{3,2,1,0:T(4,128)(2,1)} %pick.1), calls=%async_computation | async-start | bytes 262144 | tf_op jit(solution)/shard_map/all_to_all | solution.py:191
  10.0 13.4 %near.1 = (f32[4,2,4,256,256]{4,3,2,1,0:T(8,128)}, f32[4,2,4,8,256]{4,3,2,1,0:T(8,128)}) custom-call(s32[8]{0:T(128)} %counts.3, bf16[1,4,256,2048]{3,2,1,0:T(8,128)(2,1)} %q.3, bf16[1,4,256,256]{3,2,1,0:T(8,128)(2,1)} %k.1, bf16[1,4,256,256]{3,2,1,0:T(8,128)(2,1)} %v.1), custom_call_target="tpu_custom_call" | custom-call | flops 2147483648 | tf_op jit(solution)/shard_map/near/pallas_call | solution.py:201
  23.4 0.0 all-to-all-done.front
  23.4 0.0 copy-start.3
  23.4 0.6 %copy-done.3 = bf16[32,2,4,256]{3,2,1,0:T(4,128)(2,1)} copy-done((bf16[32,2,4,256]{3,2,1,0:T(4,128)(2,1)}, bf16[32,2,4,256]{3,2,1,0:T(4,128)(2,1)S(1)}, u32[]{:S(2)}) %copy-start.3) | copy-done | bytes 131096
  24.1 12.7 %far.1 = bf16[1,4,256,2048]{3,2,1,0:T(8,128)(2,1)} custom-call(s32[8]{0:T(128)} %counts.3, bf16[32,2,4,256]{3,2,1,0:T(4,128)(2,1)} %copy-done.3, bf16[1,4,256,2048]{3,2,1,0:T(8,128)(2,1)} %q.3, f32[4,2,4,256,256]{4,3,2,1,0:T(8,128)} %get-tuple-element.7.o, f32[4,2,4,8,256]{4,3,2,1,0:T(8,128)} %get-tuple-element.8.stat), custom_call_target="tpu_custom_call" | custom-call | tf_op jit(solution)/shard_map/far/pallas_call | solution.py:219
Async XLA Ops:
  0.0 0.9 %copy-start = (bf16[16,4,1024]{2,1,0:T(4,128)(2,1)S(1)}, bf16[16,4,1024]{2,1,0:T(4,128)(2,1)}, u32[]{:S(2)}) copy-start(bf16[16,4,1024]{2,1,0:T(4,128)(2,1)} %keys.1) | copy-start | bytes 393220
  0.9 0.9 %copy-start.1 = (bf16[16,4,1024]{2,1,0:T(4,128)(2,1)S(1)}, bf16[16,4,1024]{2,1,0:T(4,128)(2,1)}, u32[]{:S(2)}) copy-start(bf16[16,4,1024]{2,1,0:T(4,128)(2,1)} %values.1) | copy-start | bytes 393220
  1.8 0.7 %copy-start.2 = (s32[8]{0:T(128)S(1)}, s32[8]{0:T(128)}, u32[]{:S(2)}) copy-start(s32[8]{0:T(128)} %assign.1) | copy-start | bytes 100
  3.8 19.6 %all-to-all-start = ((bf16[32,2,4,256]{3,2,1,0:T(4,128)(2,1)}), bf16[32,2,4,256]{3,2,1,0:T(4,128)(2,1)S(1)}, u32[]{:S(2)}, u32[]{:S(2)}) async-start(bf16[32,2,4,256]{3,2,1,0:T(4,128)(2,1)} %pick.1), calls=%async_computation | async-start | bytes 262144 | tf_op jit(solution)/shard_map/all_to_all | solution.py:191
  23.4 0.6 %copy-start.3 = (bf16[32,2,4,256]{3,2,1,0:T(4,128)(2,1)}, bf16[32,2,4,256]{3,2,1,0:T(4,128)(2,1)S(1)}, u32[]{:S(2)}) copy-start(bf16[32,2,4,256]{3,2,1,0:T(4,128)(2,1)S(1)} %all-to-all-done.front) | copy-start | bytes 393220
